TPU v7x, 32 devices: a whole 2x2x4 slice. The times are simulated.
32 devices in a mesh: pair: 2 (over y), rep: 4 (over x, core), blk: 4 (over z).
Axes of the slice: x: 2, y: 2, z: 4, core: 2. Of those that a mesh axis runs over, the one named last changes fastest.
Arguments:
- src_spectra: bfloat16 [64, 8192], P(None, ('pair', 'rep', 'blk')), parts along dimension 1, may hold values from -4 to 4
- tgt_spectra: bfloat16 [64, 8192], P(None, ('pair', 'blk')), parts along dimension 1, may hold values from -4 to 4
- log_src_weight: float32 [8192], P(('pair', 'rep', 'blk')), parts along dimension 0, may hold values from -2 to 2
- log_tgt_weight: float32 [8192], P(('pair', 'blk')), parts along dimension 0, may hold values from -2 to 2
- src_potential: float32 [8192], P(('pair', 'rep', 'blk')), parts along dimension 0, may hold values from -4 to 250
- tgt_potential: float32 [8192], P(('pair', 'blk')), parts along dimension 0, may hold values from -4 to 250
Outputs:
- src_updated: float32 [8192], P(('pair', 'rep', 'blk')), parts along dimension 0
- tgt_updated: float32 [8192], P(('pair', 'blk')), parts along dimension 0
There are 2 independent parts, one for each index of `pair`. A program takes and returns all parts, laid end to end along the dimension named above; each array names one. Nothing has to cross between parts.
All inputs are finite; a program needn't handle non-finite values.
Results may differ from a plain program's by a relative error of at most 0.0003.
Values may be sent and summed in bfloat16 or wider, within the bound.
No kernel may reach another device: no remote copies, remote signals or barrier semaphores. Data moves between devices by JAX's collectives and lax.ppermute only.
A program may use at most 128 MiB of HBM per device.

v0:
```python
import jax
import jax.numpy as jnp
from jax import lax
from jax.sharding import PartitionSpec as P


def passed_along(value, axis, steps):
    count = lax.axis_size(axis)
    pairs = [(source, (source + steps) % count) for source in range(count)]
    return lax.ppermute(value, axis, pairs)


def merged(value, axis, join):
    pieces = jax.tree.map(lambda part: lax.all_gather(part, axis), value)
    head = jax.tree.map(lambda part: part[0], pieces)
    tail = jax.tree.map(lambda part: part[1:], pieces)
    so_far, _ = lax.scan(lambda so_far, share: (join(so_far, share), None), head, tail)
    return so_far


def peaks_join(earlier, later):
    joined = jnp.maximum(earlier[0], later[0])
    return (
        joined,
        earlier[1] * jnp.exp(earlier[0] - joined) + later[1] * jnp.exp(later[0] - joined),
    )


def tile_scores(src_spectra, src_square, src_bias, tgt_bias, spectra_piece, offset):
    width = spectra_piece.shape[1]
    piece_float = spectra_piece.astype(jnp.float32)
    tgt_square = 0.5 * jnp.sum(piece_float * piece_float, axis=0)
    products = lax.dot_general(
        src_spectra, spectra_piece, (((0,), (0,)), ((), ())), preferred_element_type=jnp.float32
    )
    cost_tile = src_square[:, None] + tgt_square[None, :] - products
    bias_piece = lax.dynamic_slice_in_dim(tgt_bias, offset, width, 0)
    return (bias_piece[None, :] - cost_tile, src_bias[:, None] - cost_tile)


def row_update(row_peak, row_totals, row_scores):
    joined = jnp.maximum(row_peak, jnp.max(row_scores, axis=1))
    fresh = jnp.sum(jnp.exp(row_scores - joined[:, None]), axis=1)
    return (joined, row_totals * jnp.exp(row_peak - joined) + fresh)


def column_part(col_scores):
    block_peak = jnp.max(col_scores, axis=0)
    return (block_peak, jnp.sum(jnp.exp(col_scores - block_peak[None, :]), axis=0))


def on_device(
    src_spectra, tgt_spectra, log_src_weight, log_tgt_weight, src_potential, tgt_potential
):
    src_float = src_spectra.astype(jnp.float32)
    src_square = 0.5 * jnp.sum(src_float * src_float, axis=0)
    src_bias = log_src_weight + src_potential
    tgt_bias = lax.all_gather(log_tgt_weight + tgt_potential, "blk", axis=0, tiled=True)
    own_width = tgt_spectra.shape[1]
    everything = tgt_bias.shape[0]
    rows_here = src_spectra.shape[1]
    start_peak = jnp.full((rows_here,), -jnp.inf, jnp.float32)
    start_totals = jnp.zeros((rows_here,), jnp.float32)
    shards = everything // own_width
    home = lax.axis_index("blk")

    def turn(turn_index, carry):
        row_peak, row_totals, spectra_piece, carried_peak, carried_totals = carry
        offset = (home - turn_index) % shards * own_width
        row_scores, col_scores = tile_scores(
            src_spectra, src_square, src_bias, tgt_bias, spectra_piece, offset
        )
        row_peak, row_totals = row_update(row_peak, row_totals, row_scores)
        carried_peak, carried_totals = peaks_join(
            (carried_peak, carried_totals), column_part(col_scores)
        )
        spectra_piece = passed_along(spectra_piece, "blk", 1)
        carried_peak, carried_totals = passed_along((carried_peak, carried_totals), "blk", 1)
        return (row_peak, row_totals, spectra_piece, carried_peak, carried_totals)

    carry = (
        start_peak,
        start_totals,
        tgt_spectra,
        jnp.full((own_width,), -jnp.inf, jnp.float32),
        jnp.zeros((own_width,), jnp.float32),
    )
    row_peak, row_totals, returned, carried_peak, carried_totals = lax.fori_loop(
        0, shards, turn, carry
    )
    mine_peak, mine_totals = merged((carried_peak, carried_totals), "rep", peaks_join)
    tgt_new = -(mine_peak + jnp.log(mine_totals))
    src_new = -(row_peak + jnp.log(row_totals))
    return (0.5 * (src_potential + src_new), 0.5 * (tgt_potential + tgt_new))


def solution(mesh):
    placed = (
        P(None, ("pair", "rep", "blk")),
        P(None, ("pair", "blk")),
        P(("pair", "rep", "blk")),
        P(("pair", "blk")),
        P(("pair", "rep", "blk")),
        P(("pair", "blk")),
    )
    return jax.shard_map(
        on_device,
        mesh=mesh,
        in_specs=placed,
        out_specs=(P(("pair", "rep", "blk")), P(("pair", "blk"))),
        check_vma=False,
    )
```

profile of v0, /device:TPU:0, one launch (start us, length us, event | category | flops | bytes accessed | tf_op | source)
XLA Modules:
  0.0 62.2 jit_solution(9020351512151376552)
XLA Ops:
  0.6 0.0 copy-start
  0.6 0.0 copy-start.3
  0.7 0.0 copy-start.4
  0.7 0.0 copy-start.2
  0.7 0.7 %copy-done.3 = f32[1024]{0:T(1024)S(1)} copy-done((f32[1024]{0:T(1024)S(1)}, f32[1024]{0:T(1024)}, u32[]{:S(2)}) %copy-start.3) | copy-done | bytes 4120
  1.4 0.0 copy-done.4
  1.4 14.9 %all_gather.15 = f32[4096]{0:T(1024)S(1)} all-gather(f32[1024]{0:T(1024)S(1)} %add.130), channel_id=1, replica_groups=mesh['pair'=2,'rep'=4,'blk'=4] {'blk'}, dimensions={0}, use_global_device_ids=true | all-gather | bytes 20480 | tf_op jit(solution)/shard_map/all_gather | solution.py:58
  16.3 0.0 copy-done.2
  16.3 0.0 copy-start.6
  16.3 0.0 copy-start.5
  16.4 0.7 %copy-done.6 = f32[256]{0:T(256)S(1)} copy-done((f32[256]{0:T(256)S(1)}, f32[256]{0:T(256)}, u32[]{:S(2)}) %copy-start.6) | copy-done | bytes 1048
  17.0 0.0 copy-done.5
  17.0 0.0 copy-done
  17.0 32.7 %while.37 = (s32[]{:T(128)}, f32[256]{0:T(256)S(1)}, f32[256]{0:T(256)S(1)}, bf16[64,1024]{1,0:T(8,128)(2,1)S(1)}, f32[1024]{0:T(1024)S(1)}, /*index=5*/f32[1024...) while((s32[]{:T(128)}, f32[256]{0:T(256)S(1)}, ...), condition=%wide.region_7.8_spmd.clone, body=%wide.region_1.7_spmd.clone.sunk | while | flops 36902160 | bytes 3297739 | solution.py:88
  17.1 1.6 %collective-permute-start = (bf16[64,1024]{1,0:T(8,128)(2,1)S(1)}, bf16[64,1024]{1,0:T(8,128)(2,1)S(1)}, u32[]{:S(2)}, u32[]{:S(2)}) collective-permute-start(bf16[64,1024]{1,0:T(8,128)(2,1)S(1)} %copy.17), channel_id=1, source_target_pairs={{0,1},{1,2},{2,3},{3,0},{4,5},{5,6},{6,7},{7,4},{8,9},{9,10},{10,1... | collective-permute-start | bytes 393224 | tf_op jit(solution)/shard_map/while/body/eval_jaxpr/ppermute | solution.py:10
  18.8 0.5 subtract_reduce_fusion.3
  19.3 0.4 exponential_reduce_fusion.3
  19.8 0.1 collective-permute-start.1
  19.8 2.9 %collective-permute-start.2 = (f32[1024]{0:T(1024)S(1)}, f32[1024]{0:T(1024)S(1)}, u32[]{:S(2)}, u32[]{:S(2)}) collective-permute-start(f32[1024]{0:T(1024)S(1)} %get-tuple-element.502), channel_id=1, source_target_pairs={{0,1},{1,2},{2,3},{3,0},{4,5},{5,6},{6,7},{7,4},{8,9},{9,10},{10,1... | collective-permute-start | bytes 12296 | tf_op jit(solution)/shard_map/while/body/eval_jaxpr/ppermute | solution.py:10
  22.8 2.4 %collective-permute-done.1 = f32[1024]{0:T(1024)S(1)} collective-permute-done((f32[1024]{0:T(1024)S(1)}, f32[1024]{0:T(1024)S(1)}, u32[]{:S(2)}, u32[]{:S(2)}) %collective-permute-start.1) | collective-permute-done | bytes 4128 | tf_op jit(solution)/shard_map/while/body/eval_jaxpr/ppermute | solution.py:10
  25.2 0.1 collective-permute-done.2
  25.3 0.0 collective-permute-done
  25.3 1.1 %collective-permute-start = (bf16[64,1024]{1,0:T(8,128)(2,1)S(1)}, bf16[64,1024]{1,0:T(8,128)(2,1)S(1)}, u32[]{:S(2)}, u32[]{:S(2)}) collective-permute-start(bf16[64,1024]{1,0:T(8,128)(2,1)S(1)} %copy.17), channel_id=1, source_target_pairs={{0,1},{1,2},{2,3},{3,0},{4,5},{5,6},{6,7},{7,4},{8,9},{9,10},{10,1... | collective-permute-start | bytes 393224 | tf_op jit(solution)/shard_map/while/body/eval_jaxpr/ppermute | solution.py:10
  26.5 0.5 subtract_reduce_fusion.3
  27.0 0.4 exponential_reduce_fusion.3
  27.5 0.5 collective-permute-start.1
  28.0 1.6 %collective-permute-start.2 = (f32[1024]{0:T(1024)S(1)}, f32[1024]{0:T(1024)S(1)}, u32[]{:S(2)}, u32[]{:S(2)}) collective-permute-start(f32[1024]{0:T(1024)S(1)} %get-tuple-element.502), channel_id=1, source_target_pairs={{0,1},{1,2},{2,3},{3,0},{4,5},{5,6},{6,7},{7,4},{8,9},{9,10},{10,1... | collective-permute-start | bytes 12296 | tf_op jit(solution)/shard_map/while/body/eval_jaxpr/ppermute | solution.py:10
  29.6 3.4 %collective-permute-done.1 = f32[1024]{0:T(1024)S(1)} collective-permute-done((f32[1024]{0:T(1024)S(1)}, f32[1024]{0:T(1024)S(1)}, u32[]{:S(2)}, u32[]{:S(2)}) %collective-permute-start.1) | collective-permute-done | bytes 4128 | tf_op jit(solution)/shard_map/while/body/eval_jaxpr/ppermute | solution.py:10
  33.0 0.4 collective-permute-done.2
  33.4 0.0 collective-permute-done
  33.4 0.1 collective-permute-start
  33.6 0.5 subtract_reduce_fusion.3
  34.1 0.4 exponential_reduce_fusion.3
  34.6 1.6 %collective-permute-start.1 = (f32[1024]{0:T(1024)S(1)}, f32[1024]{0:T(1024)S(1)}, u32[]{:S(2)}, u32[]{:S(2)}) collective-permute-start(f32[1024]{0:T(1024)S(1)} %get-tuple-element.501), channel_id=1, source_target_pairs={{0,1},{1,2},{2,3},{3,0},{4,5},{5,6},{6,7},{7,4},{8,9},{9,10},{10,1... | collective-permute-start | bytes 12296 | tf_op jit(solution)/shard_map/while/body/eval_jaxpr/ppermute | solution.py:10
  36.2 1.1 %collective-permute-start.2 = (f32[1024]{0:T(1024)S(1)}, f32[1024]{0:T(1024)S(1)}, u32[]{:S(2)}, u32[]{:S(2)}) collective-permute-start(f32[1024]{0:T(1024)S(1)} %get-tuple-element.502), channel_id=1, source_target_pairs={{0,1},{1,2},{2,3},{3,0},{4,5},{5,6},{6,7},{7,4},{8,9},{9,10},{10,1... | collective-permute-start | bytes 12296 | tf_op jit(solution)/shard_map/while/body/eval_jaxpr/ppermute | solution.py:10
  37.3 3.8 %collective-permute-done.1 = f32[1024]{0:T(1024)S(1)} collective-permute-done((f32[1024]{0:T(1024)S(1)}, f32[1024]{0:T(1024)S(1)}, u32[]{:S(2)}, u32[]{:S(2)}) %collective-permute-start.1) | collective-permute-done | bytes 4128 | tf_op jit(solution)/shard_map/while/body/eval_jaxpr/ppermute | solution.py:10
  41.1 0.5 collective-permute-done.2
  41.6 0.0 collective-permute-done
  41.6 0.1 collective-permute-start
  41.8 0.5 subtract_reduce_fusion.3
  42.3 0.4 exponential_reduce_fusion.3
  42.8 1.6 %collective-permute-start.1 = (f32[1024]{0:T(1024)S(1)}, f32[1024]{0:T(1024)S(1)}, u32[]{:S(2)}, u32[]{:S(2)}) collective-permute-start(f32[1024]{0:T(1024)S(1)} %get-tuple-element.501), channel_id=1, source_target_pairs={{0,1},{1,2},{2,3},{3,0},{4,5},{5,6},{6,7},{7,4},{8,9},{9,10},{10,1... | collective-permute-start | bytes 12296 | tf_op jit(solution)/shard_map/while/body/eval_jaxpr/ppermute | solution.py:10
  44.3 0.1 collective-permute-start.2
  44.4 4.1 %collective-permute-done.1 = f32[1024]{0:T(1024)S(1)} collective-permute-done((f32[1024]{0:T(1024)S(1)}, f32[1024]{0:T(1024)S(1)}, u32[]{:S(2)}, u32[]{:S(2)}) %collective-permute-start.1) | collective-permute-done | bytes 4128 | tf_op jit(solution)/shard_map/while/body/eval_jaxpr/ppermute | solution.py:10
  48.5 1.2 %collective-permute-done.2 = f32[1024]{0:T(1024)S(1)} collective-permute-done((f32[1024]{0:T(1024)S(1)}, f32[1024]{0:T(1024)S(1)}, u32[]{:S(2)}, u32[]{:S(2)}) %collective-permute-start.2) | collective-permute-done | bytes 4128 | tf_op jit(solution)/shard_map/while/body/eval_jaxpr/ppermute | solution.py:10
  49.7 0.0 collective-permute-done
  49.7 5.2 %all-gather = f32[4096]{0:T(1024)S(1)} all-gather(f32[1024]{0:T(1024)S(1)} %get-tuple-element.300), channel_id=2, replica_groups=mesh['pair'=2,'rep'=4,'blk'=4] {'rep'}, dimensions={0}, use_global_device_ids=true | all-gather | bytes 20480 | tf_op jit(solution)/shard_map/all_gather | solution.py:14
  54.9 0.0 copy-start.1
  54.9 5.2 %all-gather.1 = f32[4096]{0:T(1024)S(1)} all-gather(f32[1024]{0:T(1024)S(1)} %get-tuple-element.301), channel_id=3, replica_groups=mesh['pair'=2,'rep'=4,'blk'=4] {'rep'}, dimensions={0}, use_global_device_ids=true | all-gather | bytes 20480 | tf_op jit(solution)/shard_map/all_gather | solution.py:14
  60.2 0.0 copy-done.1
  60.2 0.0 slice-start
  60.2 0.7 %slice-done = f32[1024]{0:T(1024)S(1)} async-done(((f32[4096]{0:T(1024)}), f32[1024]{0:T(1024)S(1)}, s32[]{:S(2)}) %slice-start) | async-done | bytes 4120 | tf_op jit(solution)/shard_map/slice | solution.py:15
  60.8 0.1 while.36
  61.0 0.6 add_multiply_fusion
  61.6 0.6 add_multiply_fusion.1
  (51 shorter events, 0.5 us)
Async XLA Ops:
  0.6 16.4 %copy-start = (bf16[64,1024]{1,0:T(8,128)(2,1)S(1)}, bf16[64,1024]{1,0:T(8,128)(2,1)}, u32[]{:S(2)}) copy-start(bf16[64,1024]{1,0:T(8,128)(2,1)} %param.11) | copy-start | bytes 393220
  0.6 0.7 %copy-start.3 = (f32[1024]{0:T(1024)S(1)}, f32[1024]{0:T(1024)}, u32[]{:S(2)}) copy-start(f32[1024]{0:T(1024)} %param.15) | copy-start | bytes 12292
  0.7 0.7 %copy-start.4 = (f32[1024]{0:T(1024)S(1)}, f32[1024]{0:T(1024)}, u32[]{:S(2)}) copy-start(f32[1024]{0:T(1024)} %param.13) | copy-start | bytes 12292
  0.7 15.6 %copy-start.2 = (bf16[64,256]{1,0:T(8,128)(2,1)S(1)}, bf16[64,256]{1,0:T(8,128)(2,1)}, u32[]{:S(2)}) copy-start(bf16[64,256]{1,0:T(8,128)(2,1)} %param.10) | copy-start | bytes 98308
  16.3 0.7 %copy-start.6 = (f32[256]{0:T(256)S(1)}, f32[256]{0:T(256)}, u32[]{:S(2)}) copy-start(f32[256]{0:T(256)} %param.12) | copy-start | bytes 3076
  16.3 0.7 %copy-start.5 = (f32[256]{0:T(256)S(1)}, f32[256]{0:T(256)}, u32[]{:S(2)}) copy-start(f32[256]{0:T(256)} %param.14) | copy-start | bytes 3076
  17.1 8.2 %collective-permute-start = (bf16[64,1024]{1,0:T(8,128)(2,1)S(1)}, bf16[64,1024]{1,0:T(8,128)(2,1)S(1)}, u32[]{:S(2)}, u32[]{:S(2)}) collective-permute-start(bf16[64,1024]{1,0:T(8,128)(2,1)S(1)} %copy.17), channel_id=1, source_target_pairs={{0,1},{1,2},{2,3},{3,0},{4,5},{5,6},{6,7},{7,4},{8,9},{9,10},{10,1... | collective-permute-start | bytes 393224 | tf_op jit(solution)/shard_map/while/body/eval_jaxpr/ppermute | solution.py:10
  19.8 5.5 %collective-permute-start.1 = (f32[1024]{0:T(1024)S(1)}, f32[1024]{0:T(1024)S(1)}, u32[]{:S(2)}, u32[]{:S(2)}) collective-permute-start(f32[1024]{0:T(1024)S(1)} %get-tuple-element.501), channel_id=1, source_target_pairs={{0,1},{1,2},{2,3},{3,0},{4,5},{5,6},{6,7},{7,4},{8,9},{9,10},{10,1... | collective-permute-start | bytes 12296 | tf_op jit(solution)/shard_map/while/body/eval_jaxpr/ppermute | solution.py:10
  19.8 5.5 %collective-permute-start.2 = (f32[1024]{0:T(1024)S(1)}, f32[1024]{0:T(1024)S(1)}, u32[]{:S(2)}, u32[]{:S(2)}) collective-permute-start(f32[1024]{0:T(1024)S(1)} %get-tuple-element.502), channel_id=1, source_target_pairs={{0,1},{1,2},{2,3},{3,0},{4,5},{5,6},{6,7},{7,4},{8,9},{9,10},{10,1... | collective-permute-start | bytes 12296 | tf_op jit(solution)/shard_map/while/body/eval_jaxpr/ppermute | solution.py:10
  25.3 8.1 %collective-permute-start = (bf16[64,1024]{1,0:T(8,128)(2,1)S(1)}, bf16[64,1024]{1,0:T(8,128)(2,1)S(1)}, u32[]{:S(2)}, u32[]{:S(2)}) collective-permute-start(bf16[64,1024]{1,0:T(8,128)(2,1)S(1)} %copy.17), channel_id=1, source_target_pairs={{0,1},{1,2},{2,3},{3,0},{4,5},{5,6},{6,7},{7,4},{8,9},{9,10},{10,1... | collective-permute-start | bytes 393224 | tf_op jit(solution)/shard_map/while/body/eval_jaxpr/ppermute | solution.py:10
  27.5 5.5 %collective-permute-start.1 = (f32[1024]{0:T(1024)S(1)}, f32[1024]{0:T(1024)S(1)}, u32[]{:S(2)}, u32[]{:S(2)}) collective-permute-start(f32[1024]{0:T(1024)S(1)} %get-tuple-element.501), channel_id=1, source_target_pairs={{0,1},{1,2},{2,3},{3,0},{4,5},{5,6},{6,7},{7,4},{8,9},{9,10},{10,1... | collective-permute-start | bytes 12296 | tf_op jit(solution)/shard_map/while/body/eval_jaxpr/ppermute | solution.py:10
  28.0 5.4 %collective-permute-start.2 = (f32[1024]{0:T(1024)S(1)}, f32[1024]{0:T(1024)S(1)}, u32[]{:S(2)}, u32[]{:S(2)}) collective-permute-start(f32[1024]{0:T(1024)S(1)} %get-tuple-element.502), channel_id=1, source_target_pairs={{0,1},{1,2},{2,3},{3,0},{4,5},{5,6},{6,7},{7,4},{8,9},{9,10},{10,1... | collective-permute-start | bytes 12296 | tf_op jit(solution)/shard_map/while/body/eval_jaxpr/ppermute | solution.py:10
  33.4 8.2 %collective-permute-start = (bf16[64,1024]{1,0:T(8,128)(2,1)S(1)}, bf16[64,1024]{1,0:T(8,128)(2,1)S(1)}, u32[]{:S(2)}, u32[]{:S(2)}) collective-permute-start(bf16[64,1024]{1,0:T(8,128)(2,1)S(1)} %copy.17), channel_id=1, source_target_pairs={{0,1},{1,2},{2,3},{3,0},{4,5},{5,6},{6,7},{7,4},{8,9},{9,10},{10,1... | collective-permute-start | bytes 393224 | tf_op jit(solution)/shard_map/while/body/eval_jaxpr/ppermute | solution.py:10
  34.6 6.5 %collective-permute-start.1 = (f32[1024]{0:T(1024)S(1)}, f32[1024]{0:T(1024)S(1)}, u32[]{:S(2)}, u32[]{:S(2)}) collective-permute-start(f32[1024]{0:T(1024)S(1)} %get-tuple-element.501), channel_id=1, source_target_pairs={{0,1},{1,2},{2,3},{3,0},{4,5},{5,6},{6,7},{7,4},{8,9},{9,10},{10,1... | collective-permute-start | bytes 12296 | tf_op jit(solution)/shard_map/while/body/eval_jaxpr/ppermute | solution.py:10
  36.2 5.4 %collective-permute-start.2 = (f32[1024]{0:T(1024)S(1)}, f32[1024]{0:T(1024)S(1)}, u32[]{:S(2)}, u32[]{:S(2)}) collective-permute-start(f32[1024]{0:T(1024)S(1)} %get-tuple-element.502), channel_id=1, source_target_pairs={{0,1},{1,2},{2,3},{3,0},{4,5},{5,6},{6,7},{7,4},{8,9},{9,10},{10,1... | collective-permute-start | bytes 12296 | tf_op jit(solution)/shard_map/while/body/eval_jaxpr/ppermute | solution.py:10
  41.6 8.1 %collective-permute-start = (bf16[64,1024]{1,0:T(8,128)(2,1)S(1)}, bf16[64,1024]{1,0:T(8,128)(2,1)S(1)}, u32[]{:S(2)}, u32[]{:S(2)}) collective-permute-start(bf16[64,1024]{1,0:T(8,128)(2,1)S(1)} %copy.17), channel_id=1, source_target_pairs={{0,1},{1,2},{2,3},{3,0},{4,5},{5,6},{6,7},{7,4},{8,9},{9,10},{10,1... | collective-permute-start | bytes 393224 | tf_op jit(solution)/shard_map/while/body/eval_jaxpr/ppermute | solution.py:10
  42.8 5.7 %collective-permute-start.1 = (f32[1024]{0:T(1024)S(1)}, f32[1024]{0:T(1024)S(1)}, u32[]{:S(2)}, u32[]{:S(2)}) collective-permute-start(f32[1024]{0:T(1024)S(1)} %get-tuple-element.501), channel_id=1, source_target_pairs={{0,1},{1,2},{2,3},{3,0},{4,5},{5,6},{6,7},{7,4},{8,9},{9,10},{10,1... | collective-permute-start | bytes 12296 | tf_op jit(solution)/shard_map/while/body/eval_jaxpr/ppermute | solution.py:10
  44.3 5.4 %collective-permute-start.2 = (f32[1024]{0:T(1024)S(1)}, f32[1024]{0:T(1024)S(1)}, u32[]{:S(2)}, u32[]{:S(2)}) collective-permute-start(f32[1024]{0:T(1024)S(1)} %get-tuple-element.502), channel_id=1, source_target_pairs={{0,1},{1,2},{2,3},{3,0},{4,5},{5,6},{6,7},{7,4},{8,9},{9,10},{10,1... | collective-permute-start | bytes 12296 | tf_op jit(solution)/shard_map/while/body/eval_jaxpr/ppermute | solution.py:10
  54.9 5.2 %copy-start.1 = (f32[4096]{0:T(1024)}, f32[4096]{0:T(1024)S(1)}, u32[]{:S(2)}) copy-start(f32[4096]{0:T(1024)S(1)} %all-gather) | copy-start | bytes 49156
  60.2 0.7 %slice-start = ((f32[4096]{0:T(1024)}), f32[1024]{0:T(1024)S(1)}, s32[]{:S(2)}) async-start(f32[4096]{0:T(1024)} %copy-done.1), calls=%async_computation | async-start | bytes 8192 | tf_op jit(solution)/shard_map/slice | solution.py:15
where the time goes:
time: 62.4 us; the launch traced here: 62.2 us
  blocking collectives  25.3 us (41%)
  waiting for transfers between devices  16 us (26%)
  starting transfers between devices  12.2 us (20%)
  other arithmetic  3.3 us (5%)
  local copies, waits for them, and re-layouts  2.21 us (4%)
  matrix products  1.93 us (3%)
  between operations  0.73 us (1%)
    ppermute x12, waiting for transfers between devices, passed_along(): return lax.ppermute(value, axis, pairs)  16 us
    all_gather x1, blocking collectives, on_device(): lax.all_gather(log_tgt_weight + tgt_potential, 'blk', axis=0, tiled=True)  14.9 us
    ppermute x12, starting transfers between devices, passed_along(): return lax.ppermute(value, axis, pairs)  12.2 us
    all_gather x2, blocking collectives, merged(): pieces = jax.tree.map(lambda part: lax.all_gather(part, axis), value)  10.4 us
    dot_general x4, matrix products, tile_scores(): lax.dot_general(src_spectra, spectra_piece, (((0,), (0,)), ((), ())), pre...  1.93 us
    reduce_sum x4, other arithmetic, column_part(): jnp.sum(jnp.exp(col_scores - block_peak[None, :]), axis=0)  1.74 us
    unnamed x14, local copies, waits for them, and re-layouts  1.4 us
  transfers between devices with their start and end apart: 12, of which 8 were waited for; matrix products, arithmetic and copies ran while one was open for 6% of the time, Pallas kernels for 0%

commit v1 on v0

--- a/solution.py
+++ b/solution.py
@@ -2,6 +2,18 @@
 import jax.numpy as jnp
 from jax import lax
 from jax.sharding import PartitionSpec as P
+
+
+def doubled_up(value, axis, dim):
+    ways, here = (lax.axis_size(axis), lax.axis_index(axis))
+    grown, reach = (value, 1)
+    while reach < ways:
+        theirs = lax.ppermute(grown, axis, [(d, d ^ reach) for d in range(ways)])
+        mine_first = jnp.concatenate([grown, theirs], axis=dim)
+        theirs_first = jnp.concatenate([theirs, grown], axis=dim)
+        grown = jnp.where(here & reach == 0, mine_first, theirs_first)
+        reach = 2 * reach
+    return grown
 
 
 def passed_along(value, axis, steps):
@@ -55,7 +67,7 @@
     src_float = src_spectra.astype(jnp.float32)
     src_square = 0.5 * jnp.sum(src_float * src_float, axis=0)
     src_bias = log_src_weight + src_potential
-    tgt_bias = lax.all_gather(log_tgt_weight + tgt_potential, "blk", axis=0, tiled=True)
+    tgt_bias = doubled_up(log_tgt_weight + tgt_potential, "blk", 0)
     own_width = tgt_spectra.shape[1]
     everything = tgt_bias.shape[0]
     rows_here = src_spectra.shape[1]

time: 62.4 us -> 59.4 us (0.952)
  blocking collectives: 25.3 us -> 10.4 us
  waiting for transfers between devices: 16 us -> 22.3 us
  starting transfers between devices: 12.2 us -> 16.4 us
  local copies, waits for them, and re-layouts: 2.21 us -> 3.5 us
    all_gather x1 -> x0, blocking collectives: 14.9 us -> none  [on_device(): lax.all_gather(log_tgt_weight + tgt_potential, 'blk', axis=0, tiled=True)]
    ppermute x0 -> x2, starting transfers between devices: none -> 6.13 us  [doubled_up(): theirs = lax.ppermute(grown, axis, [(d, d ^ reach) for d in range(ways)])]
    ppermute x0 -> x2, waiting for transfers between devices: none -> 3.15 us  [doubled_up(): theirs = lax.ppermute(grown, axis, [(d, d ^ reach) for d in range(ways)])]
    ppermute x12, waiting for transfers between devices: 16 us -> 19.1 us  [passed_along(): return lax.ppermute(value, axis, pairs)]
    ppermute x12, starting transfers between devices: 12.2 us -> 10.3 us  [passed_along(): return lax.ppermute(value, axis, pairs)]
    slice x4 -> x6, local copies, waits for them, and re-layouts: 0.03 us -> 0.83 us  [merged(): tail = jax.tree.map(lambda part: part[1:], pieces)]
    unnamed x14 -> x16, local copies, waits for them, and re-layouts: 1.4 us -> 1.88 us
  transfers between devices with their start and end apart: 12 -> 14, of which waited for: 8 -> 10; matrix products, arithmetic and copies ran while one was open for 6% -> 7% of each run, Pallas kernels for 0% -> 0%
where the time goes in v1:
time: 59.4 us; the launch traced here: 59 us
  waiting for transfers between devices  22.3 us (38%)
  starting transfers between devices  16.4 us (28%)
  blocking collectives  10.4 us (18%)
  local copies, waits for them, and re-layouts  3.5 us (6%)
  other arithmetic  3.31 us (6%)
  matrix products  1.93 us (3%)
  between operations  0.72 us (1%)
    ppermute x12, waiting for transfers between devices, passed_along(): return lax.ppermute(value, axis, pairs)  19.1 us
    all_gather x2, blocking collectives, merged(): pieces = jax.tree.map(lambda part: lax.all_gather(part, axis), value)  10.4 us
    ppermute x12, starting transfers between devices, passed_along(): return lax.ppermute(value, axis, pairs)  10.3 us
    ppermute x2, starting transfers between devices, doubled_up(): theirs = lax.ppermute(grown, axis, [(d, d ^ reach) for d in range(ways)])  6.13 us
    ppermute x2, waiting for transfers between devices, doubled_up(): theirs = lax.ppermute(grown, axis, [(d, d ^ reach) for d in range(ways)])  3.15 us
    dot_general x4, matrix products, tile_scores(): lax.dot_general(src_spectra, spectra_piece, (((0,), (0,)), ((), ())), pre...  1.93 us
    unnamed x16, local copies, waits for them, and re-layouts  1.88 us
    reduce_sum x4, other arithmetic, column_part(): jnp.sum(jnp.exp(col_scores - block_peak[None, :]), axis=0)  1.74 us
  transfers between devices with their start and end apart: 14, of which 10 were waited for; matrix products, arithmetic and copies ran while one was open for 7% of the time, Pallas kernels for 0%

profile of v1, /device:TPU:0, one launch (start us, length us, event | category | flops | bytes accessed | tf_op | source)
XLA Modules:
  0.0 59.0 jit_solution(5936960070386173701)
XLA Ops:
  0.6 0.0 copy-start.5
  0.6 0.0 copy-start.4
  0.7 0.0 copy-start.3
  0.7 0.0 copy-start.6
  0.7 0.0 copy-start.7
  0.7 0.6 %copy-done.5 = f32[1024]{0:T(1024)S(1)} copy-done((f32[1024]{0:T(1024)S(1)}, f32[1024]{0:T(1024)}, u32[]{:S(2)}) %copy-start.5) | copy-done | bytes 4120
  1.3 0.0 copy-done.4
  1.3 0.0 copy-start
  1.3 3.1 %collective-permute-start.3 = (f32[1024]{0:T(1024)S(1)}, f32[1024]{0:T(1024)S(1)}, u32[]{:S(2)}, u32[]{:S(2)}) collective-permute-start(f32[1024]{0:T(1024)S(1)} %add.130), channel_id=1, source_target_pairs={{0,1},{1,0},{2,3},{3,2},{4,5},{5,4},{6,7},{7,6},{8,9},{9,8},{10,11... | collective-permute-start | bytes 12296 | tf_op jit(solution)/shard_map/ppermute | solution.py:11
  4.4 0.0 copy-done.3
  4.5 1.6 %collective-permute-done.3 = f32[1024]{0:T(1024)S(1)} collective-permute-done((f32[1024]{0:T(1024)S(1)}, f32[1024]{0:T(1024)S(1)}, u32[]{:S(2)}, u32[]{:S(2)}) %collective-permute-start.3) | collective-permute-done | bytes 4128 | tf_op jit(solution)/shard_map/ppermute | solution.py:11
  6.0 3.0 %collective-permute-start.4 = (f32[2048]{0:T(1024)S(1)}, f32[2048]{0:T(1024)S(1)}, u32[]{:S(2)}, u32[]{:S(2)}) collective-permute-start(f32[2048]{0:T(1024)S(1)} %maximum_select_fusion.1), channel_id=1, source_target_pairs={{0,2},{1,3},{2,0},{3,1},{4,6},{5,7},{6,4},{7,5},{8,10},{9,11},{10,... | collective-permute-start | bytes 24584 | tf_op jit(solution)/shard_map/ppermute | solution.py:11
  9.1 0.0 copy-done.6
  9.1 0.0 copy-done.7
  9.1 1.6 %collective-permute-done.4 = f32[2048]{0:T(1024)S(1)} collective-permute-done((f32[2048]{0:T(1024)S(1)}, f32[2048]{0:T(1024)S(1)}, u32[]{:S(2)}, u32[]{:S(2)}) %collective-permute-start.4) | collective-permute-done | bytes 8224 | tf_op jit(solution)/shard_map/ppermute | solution.py:11
  10.7 0.0 copy-done
  10.7 33.8 %while.37 = (s32[]{:T(128)}, f32[256]{0:T(256)S(1)}, f32[256]{0:T(256)S(1)}, bf16[64,1024]{1,0:T(8,128)(2,1)S(1)}, f32[1024]{0:T(1024)S(1)}, /*index=5*/f32[1024...) while((s32[]{:T(128)}, f32[256]{0:T(256)S(1)}, ...), condition=%wide.region_7.8_spmd.clone, body=%wide.region_1.7_spmd.clone.sunk | while | flops 36902160 | bytes 3297739 | solution.py:100
  10.7 2.0 %collective-permute-start = (bf16[64,1024]{1,0:T(8,128)(2,1)S(1)}, bf16[64,1024]{1,0:T(8,128)(2,1)S(1)}, u32[]{:S(2)}, u32[]{:S(2)}) collective-permute-start(bf16[64,1024]{1,0:T(8,128)(2,1)S(1)} %copy.17), channel_id=1, source_target_pairs={{0,1},{1,2},{2,3},{3,0},{4,5},{5,6},{6,7},{7,4},{8,9},{9,10},{10,1... | collective-permute-start | bytes 393224 | tf_op jit(solution)/shard_map/while/body/eval_jaxpr/ppermute | solution.py:22
  12.8 0.5 subtract_reduce_fusion.3
  13.3 0.4 exponential_reduce_fusion.3
  13.8 1.6 %collective-permute-start.1 = (f32[1024]{0:T(1024)S(1)}, f32[1024]{0:T(1024)S(1)}, u32[]{:S(2)}, u32[]{:S(2)}) collective-permute-start(f32[1024]{0:T(1024)S(1)} %get-tuple-element.501), channel_id=1, source_target_pairs={{0,1},{1,2},{2,3},{3,0},{4,5},{5,6},{6,7},{7,4},{8,9},{9,10},{10,1... | collective-permute-start | bytes 12296 | tf_op jit(solution)/shard_map/while/body/eval_jaxpr/ppermute | solution.py:22
  15.4 1.6 %collective-permute-start.2 = (f32[1024]{0:T(1024)S(1)}, f32[1024]{0:T(1024)S(1)}, u32[]{:S(2)}, u32[]{:S(2)}) collective-permute-start(f32[1024]{0:T(1024)S(1)} %get-tuple-element.502), channel_id=1, source_target_pairs={{0,1},{1,2},{2,3},{3,0},{4,5},{5,6},{6,7},{7,4},{8,9},{9,10},{10,1... | collective-permute-start | bytes 12296 | tf_op jit(solution)/shard_map/while/body/eval_jaxpr/ppermute | solution.py:22
  17.0 2.2 %collective-permute-done.1 = f32[1024]{0:T(1024)S(1)} collective-permute-done((f32[1024]{0:T(1024)S(1)}, f32[1024]{0:T(1024)S(1)}, u32[]{:S(2)}, u32[]{:S(2)}) %collective-permute-start.1) | collective-permute-done | bytes 4128 | tf_op jit(solution)/shard_map/while/body/eval_jaxpr/ppermute | solution.py:22
  19.2 1.6 %collective-permute-done.2 = f32[1024]{0:T(1024)S(1)} collective-permute-done((f32[1024]{0:T(1024)S(1)}, f32[1024]{0:T(1024)S(1)}, u32[]{:S(2)}, u32[]{:S(2)}) %collective-permute-start.2) | collective-permute-done | bytes 4128 | tf_op jit(solution)/shard_map/while/body/eval_jaxpr/ppermute | solution.py:22
  20.8 0.0 collective-permute-done
  20.8 0.1 collective-permute-start
  21.0 0.5 subtract_reduce_fusion.3
  21.5 0.4 exponential_reduce_fusion.3
  22.0 0.1 collective-permute-start.1
  22.0 1.5 %collective-permute-start.2 = (f32[1024]{0:T(1024)S(1)}, f32[1024]{0:T(1024)S(1)}, u32[]{:S(2)}, u32[]{:S(2)}) collective-permute-start(f32[1024]{0:T(1024)S(1)} %get-tuple-element.502), channel_id=1, source_target_pairs={{0,1},{1,2},{2,3},{3,0},{4,5},{5,6},{6,7},{7,4},{8,9},{9,10},{10,1... | collective-permute-start | bytes 12296 | tf_op jit(solution)/shard_map/while/body/eval_jaxpr/ppermute | solution.py:22
  23.6 4.6 %collective-permute-done.1 = f32[1024]{0:T(1024)S(1)} collective-permute-done((f32[1024]{0:T(1024)S(1)}, f32[1024]{0:T(1024)S(1)}, u32[]{:S(2)}, u32[]{:S(2)}) %collective-permute-start.1) | collective-permute-done | bytes 4128 | tf_op jit(solution)/shard_map/while/body/eval_jaxpr/ppermute | solution.py:22
  28.2 0.1 collective-permute-done.2
  28.2 0.0 collective-permute-done
  28.3 0.1 collective-permute-start
  28.4 0.5 subtract_reduce_fusion.3
  28.9 0.4 exponential_reduce_fusion.3
  29.4 2.3 %collective-permute-start.1 = (f32[1024]{0:T(1024)S(1)}, f32[1024]{0:T(1024)S(1)}, u32[]{:S(2)}, u32[]{:S(2)}) collective-permute-start(f32[1024]{0:T(1024)S(1)} %get-tuple-element.501), channel_id=1, source_target_pairs={{0,1},{1,2},{2,3},{3,0},{4,5},{5,6},{6,7},{7,4},{8,9},{9,10},{10,1... | collective-permute-start | bytes 12296 | tf_op jit(solution)/shard_map/while/body/eval_jaxpr/ppermute | solution.py:22
  31.7 0.1 collective-permute-start.2
  31.8 3.8 %collective-permute-done.1 = f32[1024]{0:T(1024)S(1)} collective-permute-done((f32[1024]{0:T(1024)S(1)}, f32[1024]{0:T(1024)S(1)}, u32[]{:S(2)}, u32[]{:S(2)}) %collective-permute-start.1) | collective-permute-done | bytes 4128 | tf_op jit(solution)/shard_map/while/body/eval_jaxpr/ppermute | solution.py:22
  35.6 1.5 %collective-permute-done.2 = f32[1024]{0:T(1024)S(1)} collective-permute-done((f32[1024]{0:T(1024)S(1)}, f32[1024]{0:T(1024)S(1)}, u32[]{:S(2)}, u32[]{:S(2)}) %collective-permute-start.2) | collective-permute-done | bytes 4128 | tf_op jit(solution)/shard_map/while/body/eval_jaxpr/ppermute | solution.py:22
  37.1 0.0 collective-permute-done
  37.1 0.1 collective-permute-start
  37.3 0.5 subtract_reduce_fusion.3
  37.8 0.4 exponential_reduce_fusion.3
  38.3 0.9 %collective-permute-start.1 = (f32[1024]{0:T(1024)S(1)}, f32[1024]{0:T(1024)S(1)}, u32[]{:S(2)}, u32[]{:S(2)}) collective-permute-start(f32[1024]{0:T(1024)S(1)} %get-tuple-element.501), channel_id=1, source_target_pairs={{0,1},{1,2},{2,3},{3,0},{4,5},{5,6},{6,7},{7,4},{8,9},{9,10},{10,1... | collective-permute-start | bytes 12296 | tf_op jit(solution)/shard_map/while/body/eval_jaxpr/ppermute | solution.py:22
  39.1 0.1 collective-permute-start.2
  39.2 4.7 %collective-permute-done.1 = f32[1024]{0:T(1024)S(1)} collective-permute-done((f32[1024]{0:T(1024)S(1)}, f32[1024]{0:T(1024)S(1)}, u32[]{:S(2)}, u32[]{:S(2)}) %collective-permute-start.1) | collective-permute-done | bytes 4128 | tf_op jit(solution)/shard_map/while/body/eval_jaxpr/ppermute | solution.py:22
  44.0 0.6 collective-permute-done.2
  44.6 0.0 collective-permute-done
  44.6 5.2 %all-gather = f32[4096]{0:T(1024)S(1)} all-gather(f32[1024]{0:T(1024)S(1)} %get-tuple-element.300), channel_id=2, replica_groups=mesh['pair'=2,'rep'=4,'blk'=4] {'rep'}, dimensions={0}, use_global_device_ids=true | all-gather | bytes 20480 | tf_op jit(solution)/shard_map/all_gather | solution.py:26
  49.8 0.0 copy-start.1
  49.8 0.6 %copy-done.1 = f32[4096]{0:T(1024)} copy-done((f32[4096]{0:T(1024)}, f32[4096]{0:T(1024)S(1)}, u32[]{:S(2)}) %copy-start.1) | copy-done | bytes 16408
  50.4 5.2 %all-gather.1 = f32[4096]{0:T(1024)S(1)} all-gather(f32[1024]{0:T(1024)S(1)} %get-tuple-element.301), channel_id=3, replica_groups=mesh['pair'=2,'rep'=4,'blk'=4] {'rep'}, dimensions={0}, use_global_device_ids=true | all-gather | bytes 20480 | tf_op jit(solution)/shard_map/all_gather | solution.py:26
  55.5 0.0 copy-start.2
  55.5 0.0 slice-start
  55.6 0.6 %copy-done.2 = f32[4096]{0:T(1024)} copy-done((f32[4096]{0:T(1024)}, f32[4096]{0:T(1024)S(1)}, u32[]{:S(2)}) %copy-start.2) | copy-done | bytes 16408
  56.1 0.1 slice-done
  56.3 0.0 slice-start.2
  56.3 0.7 %slice-done.2 = f32[3072]{0:T(1024)S(1)} async-done(((f32[4096]{0:T(1024)}), f32[3072]{0:T(1024)S(1)}, s32[]{:S(2)}) %slice-start.2) | async-done | bytes 12312 | tf_op jit(solution)/shard_map/slice | solution.py:28
  57.0 0.7 %slice-done.1 = f32[1024]{0:T(1024)S(1)} async-done(((f32[4096]{0:T(1024)}), f32[1024]{0:T(1024)S(1)}, s32[]{:S(2)}) %slice-start.1) | async-done | bytes 4120 | tf_op jit(solution)/shard_map/slice | solution.py:27
  57.7 0.0 slice-done.3
  57.7 0.1 while.36
  57.8 0.6 %add_multiply_fusion = f32[1024]{0:T(1024)} fusion(f32[1024]{0:T(1024)S(1)} %copy-done.4, f32[1024]{0:T(1024)S(1)} %get-tuple-element.302, f32[1024]{0:T(1024)S(1)} %get-tuple-element.303), kind=kLoop, calls=%fused_computation.18 | loop fusion | flops 4096 | bytes 16384 | tf_op jit(solution)/shard_map/mul | solution.py:106
  58.4 0.6 add_multiply_fusion.1
  (52 shorter events, 0.5 us)
Async XLA Ops:
  0.6 0.7 %copy-start.5 = (f32[1024]{0:T(1024)S(1)}, f32[1024]{0:T(1024)}, u32[]{:S(2)}) copy-start(f32[1024]{0:T(1024)} %param.13) | copy-start | bytes 12292
  0.6 0.7 %copy-start.4 = (f32[1024]{0:T(1024)S(1)}, f32[1024]{0:T(1024)}, u32[]{:S(2)}) copy-start(f32[1024]{0:T(1024)} %param.15) | copy-start | bytes 12292
  0.7 3.8 %copy-start.3 = (bf16[64,256]{1,0:T(8,128)(2,1)S(1)}, bf16[64,256]{1,0:T(8,128)(2,1)}, u32[]{:S(2)}) copy-start(bf16[64,256]{1,0:T(8,128)(2,1)} %param.10) | copy-start | bytes 98308
  0.7 8.4 %copy-start.6 = (f32[256]{0:T(256)S(1)}, f32[256]{0:T(256)}, u32[]{:S(2)}) copy-start(f32[256]{0:T(256)} %param.14) | copy-start | bytes 3076
  0.7 8.4 %copy-start.7 = (f32[256]{0:T(256)S(1)}, f32[256]{0:T(256)}, u32[]{:S(2)}) copy-start(f32[256]{0:T(256)} %param.12) | copy-start | bytes 3076
  1.3 9.4 %copy-start = (bf16[64,1024]{1,0:T(8,128)(2,1)S(1)}, bf16[64,1024]{1,0:T(8,128)(2,1)}, u32[]{:S(2)}) copy-start(bf16[64,1024]{1,0:T(8,128)(2,1)} %param.11) | copy-start | bytes 393220
  1.3 4.7 %collective-permute-start.3 = (f32[1024]{0:T(1024)S(1)}, f32[1024]{0:T(1024)S(1)}, u32[]{:S(2)}, u32[]{:S(2)}) collective-permute-start(f32[1024]{0:T(1024)S(1)} %add.130), channel_id=1, source_target_pairs={{0,1},{1,0},{2,3},{3,2},{4,5},{5,4},{6,7},{7,6},{8,9},{9,8},{10,11... | collective-permute-start | bytes 12296 | tf_op jit(solution)/shard_map/ppermute | solution.py:11
  6.0 4.7 %collective-permute-start.4 = (f32[2048]{0:T(1024)S(1)}, f32[2048]{0:T(1024)S(1)}, u32[]{:S(2)}, u32[]{:S(2)}) collective-permute-start(f32[2048]{0:T(1024)S(1)} %maximum_select_fusion.1), channel_id=1, source_target_pairs={{0,2},{1,3},{2,0},{3,1},{4,6},{5,7},{6,4},{7,5},{8,10},{9,11},{10,... | collective-permute-start | bytes 24584 | tf_op jit(solution)/shard_map/ppermute | solution.py:11
  10.7 10.1 %collective-permute-start = (bf16[64,1024]{1,0:T(8,128)(2,1)S(1)}, bf16[64,1024]{1,0:T(8,128)(2,1)S(1)}, u32[]{:S(2)}, u32[]{:S(2)}) collective-permute-start(bf16[64,1024]{1,0:T(8,128)(2,1)S(1)} %copy.17), channel_id=1, source_target_pairs={{0,1},{1,2},{2,3},{3,0},{4,5},{5,6},{6,7},{7,4},{8,9},{9,10},{10,1... | collective-permute-start | bytes 393224 | tf_op jit(solution)/shard_map/while/body/eval_jaxpr/ppermute | solution.py:22
  13.8 5.5 %collective-permute-start.1 = (f32[1024]{0:T(1024)S(1)}, f32[1024]{0:T(1024)S(1)}, u32[]{:S(2)}, u32[]{:S(2)}) collective-permute-start(f32[1024]{0:T(1024)S(1)} %get-tuple-element.501), channel_id=1, source_target_pairs={{0,1},{1,2},{2,3},{3,0},{4,5},{5,6},{6,7},{7,4},{8,9},{9,10},{10,1... | collective-permute-start | bytes 12296 | tf_op jit(solution)/shard_map/while/body/eval_jaxpr/ppermute | solution.py:22
  15.4 5.4 %collective-permute-start.2 = (f32[1024]{0:T(1024)S(1)}, f32[1024]{0:T(1024)S(1)}, u32[]{:S(2)}, u32[]{:S(2)}) collective-permute-start(f32[1024]{0:T(1024)S(1)} %get-tuple-element.502), channel_id=1, source_target_pairs={{0,1},{1,2},{2,3},{3,0},{4,5},{5,6},{6,7},{7,4},{8,9},{9,10},{10,1... | collective-permute-start | bytes 12296 | tf_op jit(solution)/shard_map/while/body/eval_jaxpr/ppermute | solution.py:22
  20.8 7.4 %collective-permute-start = (bf16[64,1024]{1,0:T(8,128)(2,1)S(1)}, bf16[64,1024]{1,0:T(8,128)(2,1)S(1)}, u32[]{:S(2)}, u32[]{:S(2)}) collective-permute-start(bf16[64,1024]{1,0:T(8,128)(2,1)S(1)} %copy.17), channel_id=1, source_target_pairs={{0,1},{1,2},{2,3},{3,0},{4,5},{5,6},{6,7},{7,4},{8,9},{9,10},{10,1... | collective-permute-start | bytes 393224 | tf_op jit(solution)/shard_map/while/body/eval_jaxpr/ppermute | solution.py:22
  22.0 6.2 %collective-permute-start.1 = (f32[1024]{0:T(1024)S(1)}, f32[1024]{0:T(1024)S(1)}, u32[]{:S(2)}, u32[]{:S(2)}) collective-permute-start(f32[1024]{0:T(1024)S(1)} %get-tuple-element.501), channel_id=1, source_target_pairs={{0,1},{1,2},{2,3},{3,0},{4,5},{5,6},{6,7},{7,4},{8,9},{9,10},{10,1... | collective-permute-start | bytes 12296 | tf_op jit(solution)/shard_map/while/body/eval_jaxpr/ppermute | solution.py:22
  22.0 6.2 %collective-permute-start.2 = (f32[1024]{0:T(1024)S(1)}, f32[1024]{0:T(1024)S(1)}, u32[]{:S(2)}, u32[]{:S(2)}) collective-permute-start(f32[1024]{0:T(1024)S(1)} %get-tuple-element.502), channel_id=1, source_target_pairs={{0,1},{1,2},{2,3},{3,0},{4,5},{5,6},{6,7},{7,4},{8,9},{9,10},{10,1... | collective-permute-start | bytes 12296 | tf_op jit(solution)/shard_map/while/body/eval_jaxpr/ppermute | solution.py:22
  28.3 8.9 %collective-permute-start = (bf16[64,1024]{1,0:T(8,128)(2,1)S(1)}, bf16[64,1024]{1,0:T(8,128)(2,1)S(1)}, u32[]{:S(2)}, u32[]{:S(2)}) collective-permute-start(bf16[64,1024]{1,0:T(8,128)(2,1)S(1)} %copy.17), channel_id=1, source_target_pairs={{0,1},{1,2},{2,3},{3,0},{4,5},{5,6},{6,7},{7,4},{8,9},{9,10},{10,1... | collective-permute-start | bytes 393224 | tf_op jit(solution)/shard_map/while/body/eval_jaxpr/ppermute | solution.py:22
  29.4 6.2 %collective-permute-start.1 = (f32[1024]{0:T(1024)S(1)}, f32[1024]{0:T(1024)S(1)}, u32[]{:S(2)}, u32[]{:S(2)}) collective-permute-start(f32[1024]{0:T(1024)S(1)} %get-tuple-element.501), channel_id=1, source_target_pairs={{0,1},{1,2},{2,3},{3,0},{4,5},{5,6},{6,7},{7,4},{8,9},{9,10},{10,1... | collective-permute-start | bytes 12296 | tf_op jit(solution)/shard_map/while/body/eval_jaxpr/ppermute | solution.py:22
  31.7 5.4 %collective-permute-start.2 = (f32[1024]{0:T(1024)S(1)}, f32[1024]{0:T(1024)S(1)}, u32[]{:S(2)}, u32[]{:S(2)}) collective-permute-start(f32[1024]{0:T(1024)S(1)} %get-tuple-element.502), channel_id=1, source_target_pairs={{0,1},{1,2},{2,3},{3,0},{4,5},{5,6},{6,7},{7,4},{8,9},{9,10},{10,1... | collective-permute-start | bytes 12296 | tf_op jit(solution)/shard_map/while/body/eval_jaxpr/ppermute | solution.py:22
  37.1 7.4 %collective-permute-start = (bf16[64,1024]{1,0:T(8,128)(2,1)S(1)}, bf16[64,1024]{1,0:T(8,128)(2,1)S(1)}, u32[]{:S(2)}, u32[]{:S(2)}) collective-permute-start(bf16[64,1024]{1,0:T(8,128)(2,1)S(1)} %copy.17), channel_id=1, source_target_pairs={{0,1},{1,2},{2,3},{3,0},{4,5},{5,6},{6,7},{7,4},{8,9},{9,10},{10,1... | collective-permute-start | bytes 393224 | tf_op jit(solution)/shard_map/while/body/eval_jaxpr/ppermute | solution.py:22
  38.3 5.7 %collective-permute-start.1 = (f32[1024]{0:T(1024)S(1)}, f32[1024]{0:T(1024)S(1)}, u32[]{:S(2)}, u32[]{:S(2)}) collective-permute-start(f32[1024]{0:T(1024)S(1)} %get-tuple-element.501), channel_id=1, source_target_pairs={{0,1},{1,2},{2,3},{3,0},{4,5},{5,6},{6,7},{7,4},{8,9},{9,10},{10,1... | collective-permute-start | bytes 12296 | tf_op jit(solution)/shard_map/while/body/eval_jaxpr/ppermute | solution.py:22
  39.1 5.4 %collective-permute-start.2 = (f32[1024]{0:T(1024)S(1)}, f32[1024]{0:T(1024)S(1)}, u32[]{:S(2)}, u32[]{:S(2)}) collective-permute-start(f32[1024]{0:T(1024)S(1)} %get-tuple-element.502), channel_id=1, source_target_pairs={{0,1},{1,2},{2,3},{3,0},{4,5},{5,6},{6,7},{7,4},{8,9},{9,10},{10,1... | collective-permute-start | bytes 12296 | tf_op jit(solution)/shard_map/while/body/eval_jaxpr/ppermute | solution.py:22
  49.8 0.6 %copy-start.1 = (f32[4096]{0:T(1024)}, f32[4096]{0:T(1024)S(1)}, u32[]{:S(2)}) copy-start(f32[4096]{0:T(1024)S(1)} %all-gather) | copy-start | bytes 49156
  55.5 0.6 %copy-start.2 = (f32[4096]{0:T(1024)}, f32[4096]{0:T(1024)S(1)}, u32[]{:S(2)}) copy-start(f32[4096]{0:T(1024)S(1)} %all-gather.1) | copy-start | bytes 49156
  55.5 0.7 %slice-start = ((f32[4096]{0:T(1024)}), f32[3072]{0:T(1024)S(1)}, s32[]{:S(2)}) async-start(f32[4096]{0:T(1024)} %copy-done.1), calls=%async_computation | async-start | bytes 24576 | tf_op jit(solution)/shard_map/slice | solution.py:28
  56.3 0.7 %slice-start.2 = ((f32[4096]{0:T(1024)}), f32[3072]{0:T(1024)S(1)}, s32[]{:S(2)}) async-start(f32[4096]{0:T(1024)} %copy-done.2), calls=%async_computation.2 | async-start | bytes 24576 | tf_op jit(solution)/shard_map/slice | solution.py:28
  57.0 0.7 %slice-start.1 = ((f32[4096]{0:T(1024)}), f32[1024]{0:T(1024)S(1)}, s32[]{:S(2)}) async-start(f32[4096]{0:T(1024)} %copy-done.1), calls=%async_computation.1 | async-start | bytes 8192 | tf_op jit(solution)/shard_map/slice | solution.py:27
  57.0 0.7 %slice-start.3 = ((f32[4096]{0:T(1024)}), f32[1024]{0:T(1024)S(1)}, s32[]{:S(2)}) async-start(f32[4096]{0:T(1024)} %copy-done.2), calls=%async_computation.3 | async-start | bytes 8192 | tf_op jit(solution)/shard_map/slice | solution.py:27
